TPU v7x, 512 devices: a whole 4x8x8 slice. The times are simulated.
512 devices in a mesh: batch: 64 (over z, y), cols: 8 (over x, core).
Axes of the slice: x: 4, y: 8, z: 8, core: 2. Of those that a mesh axis runs over, the one named last changes fastest.
Arguments:
- grad_up: float32 [64, 1024, 4096], P('batch', None, 'cols'), may hold values from -1.75 to 1.75
- grad_down: float32 [64, 4096, 1024], P('batch', 'cols'), may hold values from -1.75 to 1.75
- grad_query: float32 [64, 1024, 1024], P('batch', None, 'cols'), may hold values from -1.75 to 1.75
- grad_key: float32 [64, 1024, 1024], P('batch', None, 'cols'), may hold values from -1.75 to 1.75
- grad_value: float32 [64, 1024, 1024], P('batch', None, 'cols'), may hold values from -1.75 to 1.75
- grad_mixed: float32 [64, 1024, 1024], P('batch', 'cols'), may hold values from -1.75 to 1.75
- grad_norm: float32 [64, 1024], P('batch'), may hold values from -16 to 16
- weight_up: float32 [1024, 4096], P('batch', 'cols'), may hold values from -0.1875 to 0.1875
- weight_down: float32 [4096, 1024], P('cols', 'batch'), may hold values from -0.09375 to 0.09375
- weight_query: float32 [1024, 1024], P('batch', 'cols'), may hold values from -0.1875 to 0.1875
- weight_key: float32 [1024, 1024], P('batch', 'cols'), may hold values from -0.1875 to 0.1875
- weight_value: float32 [1024, 1024], P('batch', 'cols'), may hold values from -0.1875 to 0.1875
- weight_mixed: float32 [1024, 1024], P('cols', 'batch'), may hold values from -0.1875 to 0.1875
- weight_norm: float32 [1024], P('batch'), may hold values from 0.25 to 1.75
Outputs:
- copy_up: bfloat16 [1024, 4096], P(None, 'cols')
- copy_down: bfloat16 [4096, 1024], P('cols')
- copy_query: bfloat16 [1024, 1024], P(None, 'cols')
- copy_key: bfloat16 [1024, 1024], P(None, 'cols')
- copy_value: bfloat16 [1024, 1024], P(None, 'cols')
- copy_mixed: bfloat16 [1024, 1024], P('cols')
- copy_norm: bfloat16 [1024], replicated
- new_up: float32 [1024, 4096], P('batch', 'cols')
- new_down: float32 [4096, 1024], P('cols', 'batch')
- new_query: float32 [1024, 1024], P('batch', 'cols')
- new_key: float32 [1024, 1024], P('batch', 'cols')
- new_value: float32 [1024, 1024], P('batch', 'cols')
- new_mixed: float32 [1024, 1024], P('cols', 'batch')
- new_norm: float32 [1024], P('batch')
All inputs are finite; a program needn't handle non-finite values.
Results may differ from a plain program's by a relative error of at most 0.0004.
Values may be sent and summed in bfloat16 or wider, within the bound.
No kernel may reach another device: no remote copies, remote signals or barrier semaphores. Data moves between devices by JAX's collectives and lax.ppermute only.
A program may use at most 64 MiB of HBM per device.

v0:
```python
import jax
import jax.numpy as jnp
from jax import lax
from jax.sharding import PartitionSpec as P

learn_rate = 0.3


def in_blocks(x, dim, count):
    before, after = (x.shape[:dim], x.shape[dim + 1 :])
    return jnp.moveaxis(x.reshape(*before, count, -1, *after), dim, 0)


def one_scatter(arrays, axis, dims):
    count = lax.axis_size(axis)
    parts = [in_blocks(a, dim, count) for a, dim in zip(arrays, dims)]
    lines = jnp.concatenate([b.reshape(count, -1) for b in parts], axis=1)
    extent = max(16, -(-lines.shape[1] // 1024) * 8)
    lines = jnp.pad(lines, ((0, 0), (0, extent * 128 - lines.shape[1]))).reshape(-1, 128)
    flat, at, done = (lax.psum_scatter(lines, axis, tiled=True).reshape(-1), 0, [])
    for b in parts:
        part = b[0]
        done.append(flat[at : at + part.size].reshape(part.shape))
        at += part.size
    return tuple(done)


def rows_first(arrays, axis, dims):
    turned = [jnp.moveaxis(a, dim, 0) for a, dim in zip(arrays, dims)]
    widths = [t[0].size for t in turned]
    both = jnp.concatenate([t.reshape(-1, w) for t, w in zip(turned, widths)], axis=1)
    whole = lax.all_gather(both, axis, axis=0, tiled=True)
    parts = jnp.split(whole, [sum(widths[:k]) for k in range(1, len(widths))], axis=1)
    return tuple(
        (
            jnp.moveaxis(b.reshape(-1, *t.shape[1:]), 0, dim)
            for b, t, dim in zip(parts, turned, dims)
        )
    )


def shards(
    grad_up,
    grad_down,
    grad_query,
    grad_key,
    grad_value,
    grad_mixed,
    grad_norm,
    weight_up,
    weight_down,
    weight_query,
    weight_key,
    weight_value,
    weight_mixed,
    weight_norm,
):
    mean_up, mean_down, mean_query, mean_key, mean_value, mean_mixed, mean_norm = one_scatter(
        (
            grad_up[0],
            grad_down[0],
            grad_query[0],
            grad_key[0],
            grad_value[0],
            grad_mixed[0],
            grad_norm[0],
        ),
        "batch",
        (0, 1, 0, 0, 0, 1, 0),
    )
    mean_rate = lax.axis_size("batch") ** (-0.5)
    mean_up = mean_up * mean_rate
    mean_down = mean_down * mean_rate
    mean_query = mean_query * mean_rate
    mean_key = mean_key * mean_rate
    mean_value = mean_value * mean_rate
    mean_mixed = mean_mixed * mean_rate
    mean_norm = mean_norm * mean_rate
    new_up = weight_up - learn_rate * mean_up
    new_down = weight_down - learn_rate * mean_down
    new_query = weight_query - learn_rate * mean_query
    new_key = weight_key - learn_rate * mean_key
    new_value = weight_value - learn_rate * mean_value
    new_mixed = weight_mixed - learn_rate * mean_mixed
    new_norm = weight_norm - learn_rate * mean_norm
    copy_up, copy_down, copy_query, copy_key, copy_value, copy_mixed, copy_norm = rows_first(
        (
            new_up.astype(jnp.bfloat16),
            new_down.astype(jnp.bfloat16),
            new_query.astype(jnp.bfloat16),
            new_key.astype(jnp.bfloat16),
            new_value.astype(jnp.bfloat16),
            new_mixed.astype(jnp.bfloat16),
            new_norm.astype(jnp.bfloat16),
        ),
        "batch",
        (0, 1, 0, 0, 0, 1, 0),
    )
    return (
        copy_up,
        copy_down,
        copy_query,
        copy_key,
        copy_value,
        copy_mixed,
        copy_norm,
        new_up,
        new_down,
        new_query,
        new_key,
        new_value,
        new_mixed,
        new_norm,
    )


def solution(mesh):
    placed = (
        P("batch", None, "cols"),
        P("batch", "cols", None),
        P("batch", None, "cols"),
        P("batch", None, "cols"),
        P("batch", None, "cols"),
        P("batch", "cols", None),
        P("batch", None),
        P("batch", "cols"),
        P("cols", "batch"),
        P("batch", "cols"),
        P("batch", "cols"),
        P("batch", "cols"),
        P("cols", "batch"),
        P("batch"),
    )
    return jax.shard_map(
        shards,
        mesh=mesh,
        in_specs=placed,
        out_specs=(
            P(None, "cols"),
            P("cols", None),
            P(None, "cols"),
            P(None, "cols"),
            P(None, "cols"),
            P("cols", None),
            P(),
            P("batch", "cols"),
            P("cols", "batch"),
            P("batch", "cols"),
            P("batch", "cols"),
            P("batch", "cols"),
            P("cols", "batch"),
            P("batch"),
        ),
        check_vma=False,
    )
```

profile of v0, /device:TPU:4, one launch (start us, length us, event | category | flops | bytes accessed | tf_op | source)
XLA Modules:
  0.0 343.8 jit_solution(2726753529117511950)
XLA Ops:
  7.2 1.8 reshape_reshape_squeeze.12
  9.0 1.5 constant_dynamic-update-slice_fusion.6
  10.4 1.9 copy.68
  12.4 4.2 %copy.69 = f32[64,512,16]{0,2,1:T(8,128)} copy(f32[64,512,16]{1,2,0:T(8,128)S(1)} %bitcast.22) | data formatting | bytes 4194304 | tf_op jit(solution)/shard_map/transpose | solution.py:11
  16.6 2.8 copy.72
  21.2 1.9 reshape_reshape_squeeze.15
  23.1 2.0 copy.70
  25.1 1.6 copy.71
  26.7 1.1 copy.73
  29.1 1.5 constant_dynamic-update-slice_fusion.5
  30.6 1.9 constant_dynamic-update-slice_fusion.4
  32.5 1.9 constant_dynamic-update-slice_fusion.3
  36.8 6.0 %pad.4 = f32[64,25600]{1,0:T(8,128)} pad(f32[64,24592]{1,0:T(8,128)} %constant_dynamic-update-slice_fusion, f32[]{:T(128)} %constant.8.clone.1), padding=0_0x0_1008 | pad | bytes 12849156 | tf_op jit(solution)/shard_map/jit(_pad)/pad | solution.py:19
  42.8 6.4 %reshape.72 = f32[12800,128]{1,0:T(8,128)} reshape(f32[64,25600]{1,0:T(8,128)} %pad.4) | data formatting | bytes 13107200 | tf_op jit(solution)/shard_map/reshape | solution.py:19
  49.3 1.3 dynamic-slice
  51.3 184.5 %all-reduce.4.cloned.1.call-done = f32[12800,128]{1,0:T(8,128)} async-done(((f32[12800,128]{1,0:T(8,128)}), f32[12800,128]{1,0:T(8,128)}) %all-reduce.4.cloned.1.call-update) | async-done | bytes 6553616
  240.4 1.3 constant_dynamic-update-slice_fusion.11
  241.7 1.3 constant_dynamic-update-slice_fusion.10
  243.0 1.3 constant_dynamic-update-slice_fusion.9
  245.6 82.8 %all-gather.2.cloned.1.call-done = bf16[1024,1537]{1,0:T(8,128)(2,1)} async-done(((bf16[16,1537]{1,0:T(8,128)(2,1)}), bf16[1024,1537]{1,0:T(8,128)(2,1)}) %all-gather.2.cloned.1.call-update) | async-done | bytes 3147792 | tf_op jit(solution)/shard_map/all_gather | solution.py:32
  328.4 2.7 slice_bitcast_fusion
  331.0 1.3 copy.77
  332.3 2.1 slice_bitcast_fusion.1
  335.3 1.7 slice_reduce_fusion
  (53 shorter events, 12.3 us)
Async XLA Ops:
  7.2 228.5 %all-reduce.4.cloned.1.call-start = ((), (), s32[]{:S(2)}) async-start(), calls=%async_computation.1 | async-start | bytes 13107200
  12.4 7.1 %copy-start.2 = (f32[1,1024,128]{2,1,0:T(8,128)S(1)}, f32[1,1024,128]{2,1,0:T(8,128)}, u32[]{:S(2)}) copy-start(f32[1,1024,128]{2,1,0:T(8,128)} %param.16) | copy-start | bytes 1572868
  12.4 7.9 %copy-start.3 = (f32[1,1024,128]{2,1,0:T(8,128)S(1)}, f32[1,1024,128]{2,1,0:T(8,128)}, u32[]{:S(2)}) copy-start(f32[1,1024,128]{2,1,0:T(8,128)} %param.17) | copy-start | bytes 1572868
  16.6 11.8 %copy-start.11 = (f32[1,1024]{1,0:T(1,128)S(1)}, f32[1,1024]{1,0:T(1,128)}, u32[]{:S(2)}) copy-start(f32[1,1024]{1,0:T(1,128)} %param.20) | copy-start | bytes 12292
  27.8 6.6 %copy-start.1 = (f32[64,2048]{1,0:T(8,128)S(1)}, f32[64,2048]{1,0:T(8,128)}, u32[]{:S(2)}) copy-start(f32[64,2048]{1,0:T(8,128)} %reshape_reshape_squeeze.15) | copy-start | bytes 1572868
  27.8 7.5 %copy-start = (f32[64,2048]{1,0:T(8,128)S(1)}, f32[64,2048]{1,0:T(8,128)}, u32[]{:S(2)}) copy-start(f32[64,2048]{1,0:T(8,128)} %copy.73) | copy-start | bytes 1572868
  49.2 189.3 %copy-start.12 = (f32[16]{0:T(128)S(1)}, f32[16]{0:T(128)}, u32[]{:S(2)}) copy-start(f32[16]{0:T(128)} %param.27) | copy-start | bytes 196
  49.2 189.9 %copy-start.5 = (f32[16,512]{1,0:T(8,128)S(1)}, f32[16,512]{1,0:T(8,128)}, u32[]{:S(2)}) copy-start(f32[16,512]{1,0:T(8,128)} %param.21) | copy-start | bytes 98308
  49.2 190.6 %copy-start.6 = (f32[512,16]{0,1:T(8,128)S(1)}, f32[512,16]{0,1:T(8,128)}, u32[]{:S(2)}) copy-start(f32[512,16]{0,1:T(8,128)} %param.22) | copy-start | bytes 98308
  49.2 191.2 %copy-start.7 = (f32[16,128]{1,0:T(8,128)S(1)}, f32[16,128]{1,0:T(8,128)}, u32[]{:S(2)}) copy-start(f32[16,128]{1,0:T(8,128)} %param.23) | copy-start | bytes 24580
  49.2 192.5 %copy-start.8 = (f32[16,128]{1,0:T(8,128)S(1)}, f32[16,128]{1,0:T(8,128)}, u32[]{:S(2)}) copy-start(f32[16,128]{1,0:T(8,128)} %param.24) | copy-start | bytes 24580
  49.2 193.8 %copy-start.9 = (f32[16,128]{1,0:T(8,128)S(1)}, f32[16,128]{1,0:T(8,128)}, u32[]{:S(2)}) copy-start(f32[16,128]{1,0:T(8,128)} %param.25) | copy-start | bytes 24580
  49.2 195.1 %copy-start.10 = (f32[128,16]{0,1:T(8,128)S(1)}, f32[128,16]{0,1:T(8,128)}, u32[]{:S(2)}) copy-start(f32[128,16]{0,1:T(8,128)} %param.26) | copy-start | bytes 24580
  49.3 279.1 %all-gather.2.cloned.1.call-start = ((), (), s32[]{:S(2)}) async-start(), calls=%async_computation | async-start | bytes 3461120 | tf_op jit(solution)/shard_map/all_gather | solution.py:32
  244.9 0.6 copy-start.4
Sparse Core Ops, SparseCore 0:
  49.4 186.2 all-reduce.3
  245.7 82.6 all-gather.1
where the time goes:
time: 345 us; the launch traced here: 344 us
  waiting for transfers between devices  267 us (77%)
  local copies, waits for them, and re-layouts  53.1 us (15%)
  between operations  14.9 us (4%)
  other arithmetic  8.46 us (2%)
    unnamed x3, waiting for transfers between devices  184 us
    all_gather x1, waiting for transfers between devices, rows_first(): whole = lax.all_gather(both, axis, axis=0, tiled=True)  82.8 us
    unnamed x38, local copies, waits for them, and re-layouts  17.1 us
  transfers between devices with their start and end apart: 2, of which 2 were waited for; matrix products, arithmetic and copies ran while one was open for 0% of the time, Pallas kernels for 0%

commit v1 on v0

v1 whole, which is shorter than its diff:
```python
import jax
import jax.numpy as jnp
from jax import lax
from jax.experimental import pallas as pl
from jax.experimental.pallas import tpu as pltpu
from jax.sharding import PartitionSpec as P

learn_rate = 0.3
AX = ("batch", "cols")
N = 8
T = 12
ROWS = T * 128 + 8
PART = T * 16 + 8
anywhere = pl.BlockSpec(memory_space=pl.ANY)
in_vmem = pl.BlockSpec(memory_space=pltpu.VMEM)


def groups(swap):
    found = []
    for c in range(8):
        for o in range(N):
            along_y = (c % 2 == 0) != swap
            found.append([((o * N + k) if along_y else (k * N + o)) * 8 + c for k in range(N)])
    return found


def exchange(x, swap):
    return lax.all_to_all(x, AX, 0, 0, axis_index_groups=groups(swap))


def core():
    return lax.axis_index("cols") % 2


def pack_body(up, down, q, k, v, mixed, norm, out, down_v, mixed_v, sems, tsems):
    c = core()
    loads = [
        pltpu.make_async_copy(down, down_v, tsems.at[0]),
        pltpu.make_async_copy(mixed, mixed_v, tsems.at[1]),
    ]
    for one in loads:
        one.start()

    def copies(first):
        for f in range(N):
            at = 0
            for a in (up, q, k, v):
                for t in range(a.shape[-1] // 128):
                    lanes = pl.ds(t * 128, 128)
                    src = a.at[:, f, :, lanes] if first else a.at[f, :, :, lanes]
                    row = (at if a is up else at + 4) * 128
                    yield pltpu.make_async_copy(src, out.at[f, pl.ds(row, 128)].reshape(N, 16, 128), sems)
                    at += 1

    @pl.when(c == 0)
    def _():
        for one in copies(True):
            one.start()

    @pl.when(c == 1)
    def _():
        for one in copies(False):
            one.start()

    out[:, T * 128 :, :] = norm[...]
    for one in loads:
        one.wait()
    for src, t0, n in ((down_v, 4, 4), (mixed_v, 11, 1)):
        for z in range(N):
            for t in range(n):
                tile = src[t * 128 : (t + 1) * 128, z * 128 : (z + 1) * 128].T
                for y in range(N):
                    f = jnp.where(c == 0, y, z)
                    s = jnp.where(c == 0, z, y)
                    row = pl.multiple_of((t0 + t) * 128 + s * 16, 16)
                    out[f, pl.ds(row, 16), :] = tile[y * 16 : (y + 1) * 16]

    for one in copies(False):
        one.wait()


def pack(up, down, q, k, v, mixed, norm):
    split = [a.reshape(N, N, 16, a.shape[-1]) for a in (up, q, k, v)]
    return pl.pallas_call(
        pack_body,
        name="pack",
        out_shape=jax.ShapeDtypeStruct((N, ROWS, 128), jnp.float32),
        in_specs=[anywhere] * 6 + [in_vmem],
        out_specs=in_vmem,
        scratch_shapes=[
            pltpu.VMEM(down.shape, jnp.float32),
            pltpu.VMEM(mixed.shape, jnp.float32),
            pltpu.SemaphoreType.DMA,
            pltpu.SemaphoreType.DMA((2,)),
        ],
    )(split[0], down, *split[1:], mixed, norm)


def middle_body(got, out):
    for t in range(T):
        rows = pl.ds(t * 128, 128)
        total = got[0, rows]
        for f in range(1, N):
            total += got[f, rows]
        out[:, t * 16 : (t + 1) * 16, :] = total.reshape(N, 16, 128)
    norm = got[0, T * 128 :]
    for f in range(1, N):
        norm += got[f, T * 128 :]
    out[:, T * 16 :, :] = jnp.broadcast_to(norm[:, None, :], (N, 8, 128))


def middle(got):
    return pl.pallas_call(
        middle_body,
        name="middle",
        out_shape=jax.ShapeDtypeStruct((N, PART, 128), jnp.float32),
        in_specs=[in_vmem],
        out_specs=in_vmem,
    )(got)


def update_body(rate, got, up, down, q, k, v, mixed, norm, n_up, n_down, n_q, n_k, n_v, n_mixed, n_norm, copies):
    def step(t, weight):
        rows = pl.ds(t * 16, 16)
        total = got[0, rows]
        for s in range(1, N):
            total += got[s, rows]
        new = weight - learn_rate * (total * rate)
        copies[:, rows] = jnp.broadcast_to(new.astype(jnp.bfloat16)[None], (N, 16, 128))
        return new

    for t in range(4):
        lanes = slice(t * 128, (t + 1) * 128)
        n_up[:, lanes] = step(t, up[:, lanes])
        n_down[lanes, :] = step(4 + t, down[lanes, :].T).T
    n_q[...] = step(8, q[...])
    n_k[...] = step(9, k[...])
    n_v[...] = step(10, v[...])
    n_mixed[...] = step(11, mixed[...].T).T
    total = got[0, T * 16 :]
    for s in range(1, N):
        total += got[s, T * 16 :]
    new = norm[...] - learn_rate * (total * rate)
    n_norm[...] = new
    copies[:, T * 16 :] = jnp.broadcast_to(new.astype(jnp.bfloat16)[None], (N, 8, 128))


def update(got, weights):
    shapes = [jax.ShapeDtypeStruct(w.shape, jnp.float32) for w in weights]
    rate = REPLICAS_RATE
    return pl.pallas_call(
        lambda *refs: update_body(rate, *refs),
        name="update",
        out_shape=shapes + [jax.ShapeDtypeStruct((N, PART, 128), jnp.bfloat16)],
        in_specs=[in_vmem] * 8,
        out_specs=[in_vmem] * 8,
    )(got, *weights)


REPLICAS_RATE = 64 ** (-0.5)


def unpack_body(got, up, down, q, k, v, mixed, got_v, sems, tsem):
    c = core()
    load = pltpu.make_async_copy(got, got_v, tsem)
    load.start()

    def copies(first):
        for f in range(N):
            for a, t0 in ((up, 0), (q, 8), (k, 9), (v, 10)):
                for t in range(a.shape[-1] // 128):
                    lanes = pl.ds(t * 128, 128)
                    dst = a.at[:, f, :, lanes] if first else a.at[f, :, :, lanes]
                    yield pltpu.make_async_copy(got.at[f, :, pl.ds((t0 + t) * 16, 16)], dst, sems)

    @pl.when(c == 0)
    def _():
        for one in copies(True):
            one.start()

    @pl.when(c == 1)
    def _():
        for one in copies(False):
            one.start()

    load.wait()
    for dst, t0, n in ((down, 4, 4), (mixed, 11, 1)):
        for z in range(N):
            for t in range(n):
                rows = pl.ds((t0 + t) * 16, 16)
                parts = [got_v[jnp.where(c == 0, y, z), jnp.where(c == 0, z, y), rows] for y in range(N)]
                dst[t * 128 : (t + 1) * 128, z * 128 : (z + 1) * 128] = jnp.concatenate(parts).T

    for one in copies(False):
        one.wait()


def unpack(got):
    def out(*shape):
        return jax.ShapeDtypeStruct(shape, jnp.bfloat16)

    up, down, q, k, v, mixed = pl.pallas_call(
        unpack_body,
        name="unpack",
        out_shape=[out(N, N, 16, 512), out(512, 1024)] + [out(N, N, 16, 128)] * 3 + [out(128, 1024)],
        in_specs=[anywhere],
        out_specs=[anywhere, in_vmem] + [anywhere] * 3 + [in_vmem],
        scratch_shapes=[pltpu.VMEM(got.shape, jnp.bfloat16), pltpu.SemaphoreType.DMA, pltpu.SemaphoreType.DMA],
    )(got)
    flat = [a.reshape(1024, -1) for a in (up, q, k, v)]
    return flat[0], down, *flat[1:], mixed


def by_core(x):
    return jnp.where(core() == 0, jnp.swapaxes(x, 0, 1), x)


def shards(g_up, g_down, g_q, g_k, g_v, g_mixed, g_norm, up, down, q, k, v, mixed, norm):
    tile = jnp.pad(by_core(g_norm[0].reshape(N, N, 16)), ((0, 0), (0, 0), (0, 112)))
    chunks = pack(g_up[0], g_down[0], g_q[0], g_k[0], g_v[0], g_mixed[0], tile)
    got = exchange(middle(exchange(chunks, False)), True)
    norm_tile = jnp.broadcast_to(jnp.pad(norm, (0, 112)), (8, 128))
    *new, mine = update(got, (up, down, q, k, v, mixed, norm_tile))
    near = exchange(mine, True)
    whole = exchange(jnp.broadcast_to(near[None], (N, *near.shape)), False)
    copies = unpack(whole)
    copy_norm = by_core(whole[:, :, T * 16, :16]).reshape(1024)
    return (*copies, copy_norm, *new[:6], new[6][0, :16])


def solution(mesh):
    placed = (
        P("batch", None, "cols"),
        P("batch", "cols", None),
        P("batch", None, "cols"),
        P("batch", None, "cols"),
        P("batch", None, "cols"),
        P("batch", "cols", None),
        P("batch", None),
        P("batch", "cols"),
        P("cols", "batch"),
        P("batch", "cols"),
        P("batch", "cols"),
        P("batch", "cols"),
        P("cols", "batch"),
        P("batch"),
    )
    whole = (P(None, "cols"), P("cols", None), P(None, "cols"), P(None, "cols"), P(None, "cols"), P("cols", None), P())
    return jax.shard_map(shards, mesh=mesh, in_specs=placed, out_specs=whole + placed[7:], check_vma=False)
```

time: 345 us -> 250 us (0.72)
  waiting for transfers between devices: 267 us -> 54.3 us
  blocking collectives: 0 us -> 98.1 us
  Pallas kernels: 0 us -> 70.4 us
  local copies, waits for them, and re-layouts: 53.1 us -> 10.9 us
  between operations: 14.9 us -> 0.72 us
  starting transfers between devices: 0.08 us -> 14.1 us
  other arithmetic: 8.46 us -> 1.37 us
    unnamed x3 -> x0, waiting for transfers between devices: 184 us -> none
    all_to_all x0 -> x2, blocking collectives: none -> 98.1 us  [exchange(): return lax.all_to_all(x, AX, 0, 0, axis_index_groups=groups(swap))]
    all_gather x1 -> x0, waiting for transfers between devices: 82.8 us -> none  [rows_first(): whole = lax.all_gather(both, axis, axis=0, tiled=True)]
    pallas_call x0 -> x4, Pallas kernels: none -> 70.4 us  [the longest x1 57.8 us: unpack(): pl.pallas_call(unpack_body, name='unpack', out_shape=[out(N, N, 16, 512),...]
    all_to_all x0 -> x2, waiting for transfers between devices: none -> 54.3 us  [exchange(): return lax.all_to_all(x, AX, 0, 0, axis_index_groups=groups(swap))]
    all_to_all x0 -> x2, starting transfers between devices: none -> 14.1 us  [exchange(): return lax.all_to_all(x, AX, 0, 0, axis_index_groups=groups(swap))]
    unnamed x38 -> x17, local copies, waits for them, and re-layouts: 17.1 us -> 5.44 us
    reshape x5 -> x1, local copies, waits for them, and re-layouts: 11.3 us -> 0.8 us  [shards(): copy_norm = by_core(whole[:, :, T * 16, :16]).reshape(1024)]
  transfers between devices with their start and end apart: 2 -> 2, of which waited for: 2 -> 2; matrix products, arithmetic and copies ran while one was open for 0% -> 2% of each run, Pallas kernels for 0% -> 0%
where the time goes in v1:
time: 250 us
  blocking collectives  98.1 us (39%)
  Pallas kernels  70.4 us (28%)
  waiting for transfers between devices  54.3 us (22%)
  starting transfers between devices  14.1 us (6%)
  local copies, waits for them, and re-layouts  10.9 us (4%)
    all_to_all x2, blocking collectives, exchange(): return lax.all_to_all(x, AX, 0, 0, axis_index_groups=groups(swap))  98.1 us
    pallas_call x1, Pallas kernels, unpack(): pl.pallas_call(unpack_body, name='unpack', out_shape=[out(N, N, 16, 512),...  57.8 us
    all_to_all x2, waiting for transfers between devices, exchange(): return lax.all_to_all(x, AX, 0, 0, axis_index_groups=groups(swap))  54.3 us
    all_to_all x2, starting transfers between devices, exchange(): return lax.all_to_all(x, AX, 0, 0, axis_index_groups=groups(swap))  14.1 us
    pallas_call x1, Pallas kernels, pack(): pl.pallas_call(pack_body, name='pack', out_shape=jax.ShapeDtypeStruct((N,...  6.18 us
    unnamed x17, local copies, waits for them, and re-layouts  5.44 us
  transfers between devices with their start and end apart: 2, of which 2 were waited for; matrix products, arithmetic and copies ran while one was open for 2% of the time, Pallas kernels for 0%

profile of v1, /device:TPU:4, one launch (start us, length us, event | category | flops | bytes accessed | tf_op | source)
XLA Modules:
  0.0 249.8 jit_solution(6473429946899013913)
XLA Ops:
  0.7 0.5 broadcast.9
  1.2 1.3 reduce.3
  2.5 0.1 reshape_squeeze.19
  2.6 0.6 pad.8.norm
  3.2 6.2 %pack.1 = f32[8,1544,128]{2,1,0:T(8,128)} custom-call(f32[8,8,16,512]{3,2,1,0:T(8,128)} %bitcast.19, f32[512,1024]{1,0:T(8,128)} %bitcast.20, f32[8,8,16,128]{3,2,1,0:T(8,128)} %bitcast.21, f32[8,8,16,128]{3,2,1,0:T(8,128)} %bitcast.22, f32[8,8,16,128]{3,2,1,0:T(8,128)} %bitcast.23, f32[128,1024]{1,0:T(8,128)} %bitcast.24, f32[8,8,128]{2,1,0:T(8,128)} %pad.8.norm), custom_call_target="tpu_custom_call" | custom-call | tf_op jit(solution)/shard_map/pack/pallas_call | solution.py:84
  9.4 82.7 %all_to_all.20.got = f32[8,1544,128]{2,1,0:T(8,128)} all-to-all(f32[8,1544,128]{2,1,0:T(8,128)} %pack.1), channel_id=1, replica_groups={{0,8,16,24,32,40,48,56},{64,72,80,88,96,104,112,120},{128,136,144,152,1..., dimensions={0} | all-to-all | bytes 12648448 | tf_op jit(solution)/shard_map/all_to_all | solution.py:28
  92.1 4.0 %middle.1 = f32[8,200,128]{2,1,0:T(8,128)} custom-call(f32[8,1544,128]{2,1,0:T(8,128)} %all_to_all.20.got), custom_call_target="tpu_custom_call" | custom-call | tf_op jit(solution)/shard_map/middle/pallas_call | solution.py:113
  96.1 10.3 %all-to-all-start.1 = ((f32[8,200,128]{2,1,0:T(8,128)}), f32[8,200,128]{2,1,0:T(8,128)S(1)}, u32[]{:S(2)}, u32[]{:S(2)}) async-start(f32[8,200,128]{2,1,0:T(8,128)} %middle.1), calls=%async_computation.1 | async-start | bytes 1638400 | tf_op jit(solution)/shard_map/all_to_all | solution.py:28
  106.4 0.8 copy.35.refs_2_
  107.2 0.7 copy.36.refs_6_
  108.0 14.9 %all-to-all-done.1.refs_0_ = f32[8,200,128]{2,1,0:T(8,128)S(1)} async-done(((f32[8,200,128]{2,1,0:T(8,128)}), f32[8,200,128]{2,1,0:T(8,128)S(1)}, u32[]{:S(2)}, u32[]{:S(2)}) %all-to-all-start.1) | async-done | bytes 819232 | tf_op jit(solution)/shard_map/all_to_all | solution.py:28
  122.9 0.6 broadcast_in_dim.4.refs_7_
  123.5 0.3 copy-done.1
  123.8 2.4 update.1
  126.2 15.4 %all_to_all.21 = bf16[8,200,128]{2,1,0:T(8,128)(2,1)S(1)} all-to-all(bf16[8,200,128]{2,1,0:T(8,128)(2,1)} %get-tuple-element.28), channel_id=1, replica_groups={{0,64,128,192,256,320,384,448},{8,72,136,200,264,328,392,456},{16,80,14..., dimensions={0} | all-to-all | bytes 819200 | tf_op jit(solution)/shard_map/all_to_all | solution.py:28
  141.6 2.1 broadcast_in_dim.10
  143.7 3.8 %all-to-all-start.3 = ((bf16[8,8,200,128]{3,2,1,0:T(8,128)(2,1)}), bf16[8,8,200,128]{3,2,1,0:T(8,128)(2,1)S(1)}, u32[]{:S(2)}, u32[]{:S(2)}) async-start(bf16[8,8,200,128]{3,2,1,0:T(8,128)(2,1)} %broadcast_in_dim.10), calls=%async_computation.3 | async-start | bytes 6553600 | tf_op jit(solution)/shard_map/all_to_all | solution.py:28
  147.6 0.7 copy.38
  148.3 1.5 copy.39
  149.8 1.2 slice_bitcast_fusion
  151.0 39.4 %all-to-all-done.3.got = bf16[8,8,200,128]{3,2,1,0:T(8,128)(2,1)S(1)} async-done(((bf16[8,8,200,128]{3,2,1,0:T(8,128)(2,1)}), bf16[8,8,200,128]{3,2,1,0:T(8,128)(2,1)S(1)}, u32[]{:S(2)}, u32[]{:S(2)}) %all-to-all-start.3) | async-done | bytes 3276832 | tf_op jit(solution)/shard_map/all_to_all | solution.py:28
  190.4 0.8 reshape.48
  191.2 0.8 copy-done
  192.0 57.8 %unpack.1 = (bf16[8,8,16,512]{3,2,1,0:T(8,128)(2,1)}, bf16[512,1024]{1,0:T(8,128)(2,1)}, bf16[8,8,16,128]{3,2,1,0:T(8,128)(2,1)}, bf16[8,8,16,128]{3,2,1,0:T(8,1...) custom-call(bf16[8,8,200,128]{3,2,1,0:T(8,128)(2,1)} %copy-done), custom_call_target="tpu_custom_call" | custom-call | tf_op jit(solution)/shard_map/unpack/pallas_call | solution.py:202
  (14 shorter events, 0.1 us)
Async XLA Ops:
  92.1 14.3 %copy-start.3 = (f32[512,16]{0,1:T(8,128)S(1)}, f32[512,16]{0,1:T(8,128)}, u32[]{:S(2)}) copy-start(f32[512,16]{0,1:T(8,128)} %param.22) | copy-start | bytes 98308
  92.1 15.1 %copy-start.4 = (f32[128,16]{0,1:T(8,128)S(1)}, f32[128,16]{0,1:T(8,128)}, u32[]{:S(2)}) copy-start(f32[128,16]{0,1:T(8,128)} %param.26) | copy-start | bytes 24580
  92.1 15.9 %copy-start.5 = (f32[16]{0:T(128)S(1)}, f32[16]{0:T(128)}, u32[]{:S(2)}) copy-start(f32[16]{0:T(128)} %param.27) | copy-start | bytes 196
  96.1 26.8 %all-to-all-start.1 = ((f32[8,200,128]{2,1,0:T(8,128)}), f32[8,200,128]{2,1,0:T(8,128)S(1)}, u32[]{:S(2)}, u32[]{:S(2)}) async-start(f32[8,200,128]{2,1,0:T(8,128)} %middle.1), calls=%async_computation.1 | async-start | bytes 1638400 | tf_op jit(solution)/shard_map/all_to_all | solution.py:28
  122.9 0.9 copy-start.1
  143.7 3.8 %copy-start.2 = (f32[512,16]{1,0:T(8,128)S(1)}, f32[512,16]{1,0:T(8,128)}, u32[]{:S(2)}) copy-start(f32[512,16]{1,0:T(8,128)} %get-tuple-element.64) | copy-start | bytes 98308
  143.7 46.6 %all-to-all-start.3 = ((bf16[8,8,200,128]{3,2,1,0:T(8,128)(2,1)}), bf16[8,8,200,128]{3,2,1,0:T(8,128)(2,1)S(1)}, u32[]{:S(2)}, u32[]{:S(2)}) async-start(bf16[8,8,200,128]{3,2,1,0:T(8,128)(2,1)} %broadcast_in_dim.10), calls=%async_computation.3 | async-start | bytes 6553600 | tf_op jit(solution)/shard_map/all_to_all | solution.py:28
  190.3 1.7 copy-start
